TPU v7x, 32 devices: a whole 2x2x4 slice. The times are simulated.
32 devices in a mesh: row: 4 (over y, x), col: 8 (over z, core).
Axes of the slice: x: 2, y: 2, z: 4, core: 2. Of those that a mesh axis runs over, the one named last changes fastest.
Arguments:
- charge: float32 [256, 256, 256], P('col', 'row'), may hold values from -6 to 6
- green_spectrum: float32 [512, 512, 512], P('row', 'col'), may hold values from 0.2 to 2
Outputs:
- potential: float32 [256, 256, 256], P('col', 'row')
All inputs are finite; a program needn't handle non-finite values.
Results may differ from a plain program's by a relative error of at most 0.00007.
Values sent between devices are 32-bit elements; how exact they have to be, the bound alone decides.
A program may use at most 192 MiB of HBM per device.

v0:
```python
import math
import jax
import jax.numpy as jnp
from jax import lax
from jax.sharding import PartitionSpec as P

M = 512
N = 256


def phases(count_in, count_out, length):
    row_ids = lax.iota(jnp.int32, count_in)[:, None]
    col_ids = lax.iota(jnp.int32, count_out)[None, :]
    turn_ids = row_ids * col_ids % length
    angles = turn_ids.astype(jnp.float32) * (2.0 * math.pi / length)
    return (jnp.cos(angles), jnp.sin(angles))


def forward_table(count_in, count_out, length):
    cosine, sine_part = phases(count_in, count_out, length)
    return jnp.stack([jnp.stack([cosine, -sine_part], 1), jnp.stack([sine_part, cosine], 1)], 0)


def inverse_table(count_in, count_out, length):
    cosine, sine_part = phases(count_in, count_out, length)
    scaling = 1.0 / length
    return (
        jnp.stack([jnp.stack([cosine, sine_part], 1), jnp.stack([-sine_part, cosine], 1)], 0)
        * scaling
    )


def contract(pattern, left_side, right_side):
    return jnp.einsum(
        pattern,
        left_side,
        right_side,
        precision=lax.Precision.HIGH,
        preferred_element_type=jnp.float32,
    )


def on_device(charge, green_spectrum):
    cosine, sine_part = phases(N, M, M)
    real_table = jnp.stack([cosine, -sine_part], 1)
    along_z = contract("xyz,zqk->xyqk", charge, real_table)
    by_rows = lax.all_to_all(along_z, "row", split_axis=3, concat_axis=1, tiled=True)
    forward = forward_table(N, M, M)
    along_y = contract("xypk,pyqb->xkqb", by_rows, forward)
    spectrum = contract(
        "xkpj,pxqa->kjqa",
        lax.all_to_all(along_y, "col", split_axis=3, concat_axis=0, tiled=True),
        forward,
    )
    product = spectrum * green_spectrum[:, :, None, :]
    back_table = inverse_table(M, N, M)
    back_cos, back_sin = phases(M, N, M)
    real_back = jnp.stack([back_cos, -back_sin], 0) * (1.0 / M)
    back_x = contract("kjqa,qapx->kjpx", product, back_table)
    by_cols = lax.all_to_all(back_x, "col", split_axis=3, concat_axis=1, tiled=True)
    back_y = contract("kbpx,pbqy->kxqy", by_cols, back_table)
    return contract(
        "cxpy,pcz->xyz",
        lax.all_to_all(back_y, "row", split_axis=3, concat_axis=0, tiled=True),
        real_back,
    )


def solution(mesh):
    in_specs = (P("col", "row", None), P("row", "col", None))
    out_specs = P("col", "row", None)
    return jax.shard_map(
        on_device, mesh=mesh, in_specs=in_specs, out_specs=out_specs, check_vma=False
    )
```

profile of v0, /device:TPU:0, one launch (start us, length us, event | category | flops | bytes accessed | tf_op | source)
XLA Modules:
  0.0 1271.5 jit_solution(5702876776140178700)
XLA Ops:
  0.0 2.1 fusion.58
  2.1 5.7 convolution_bitcast_fusion.1
  7.8 16.3 %copy.38 = f32[32,64,2,512]{1,0,2,3:T(8,128)} copy(f32[32,64,2,512]{3,1,0,2:T(8,128)} %convolution_bitcast_fusion.1) | data formatting | bytes 16777216 | tf_op jit(solution)/shard_map/xyz,zqk->xyqk/dot_general | solution.py:34
  24.1 14.3 %reshape.237 = f32[4,1,524288]{2,1,0:T(1,128)} reshape(f32[512,2,32,64]{3,2,1,0:T(8,128)} %bitcast.92) | data formatting | bytes 16777216
  38.5 5.8 all-to-all-start
  44.3 1.9 fusion.57
  46.5 91.6 %all-to-all-done = f32[4,1,524288]{2,1,0:T(1,128)} async-done(((f32[4,1,524288]{2,1,0:T(1,128)}), f32[4,1,524288]{2,1,0:T(1,128)}, u32[]{:S(2)}, u32[]{:S(2)}) %all-to-all-start) | async-done | bytes 8388640 | tf_op jit(solution)/shard_map/all_to_all | solution.py:47
  138.6 28.2 %reduce = f32[4,524288]{1,0:T(4,128)} reduce(f32[4,1,524288]{2,1,0:T(1,128)} %all-to-all-done, f32[]{:T(128)} %broadcast.343), dimensions={1}, to_apply=%all_to_all.52.reduce_sub_computation | reduce | bytes 16777220 | tf_op jit(solution)/shard_map/all_to_all | solution.py:47
  166.8 16.8 %reshape.238 = f32[512,2,32,64]{3,2,1,0:T(8,128)} reshape(f32[4,524288]{1,0:T(4,128)} %reduce) | data formatting | bytes 16777216
  183.6 12.8 %copy.67 = f32[32,64,2,4,128]{4,3,1,2,0:T(4,128)} copy(f32[32,64,2,4,128]{1,0,2,4,3:T(8,128)} %bitcast.93) | data formatting | bytes 16777216 | tf_op jit(solution)/shard_map/all_to_all | solution.py:47
  196.4 4.7 copy.40
  201.1 16.9 %convolution_bitcast_fusion = f32[32,128,2,512]{3,1,2,0:T(8,128)} fusion(f32[32,256,2,128,1]{3,1,2,4,0:T(8,128)S(1)} %bitcast.99, f32[1,256,2,512]{3,1,2,0:T(8,128)S(1)} %get-tuple-element.8, f32[1,256,2,512]{3,1,2,0:T(8,128)S(1)} %get-tuple-element.7), kind=kOutput, calls=%fused_computation.9 | convolution fusion | flops 12885426176 | bytes 27262976 | tf_op jit(solution)/shard_map/xypk,pyqb->xkqb/dot_general | solution.py:34
  218.0 25.1 %copy.43 = f32[32,128,2,512]{1,2,0,3:T(2,128)} copy(f32[32,128,2,512]{3,1,2,0:T(8,128)} %convolution_bitcast_fusion) | data formatting | bytes 33554432 | tf_op jit(solution)/shard_map/xypk,pyqb->xkqb/dot_general | solution.py:34
  243.0 5.7 all-to-all-start.1
  248.8 17.7 %copy.48 = f32[128,64,512]{2,0,1:T(8,128)} copy(f32[128,64,512]{2,1,0:T(8,128)} %param.3) | data formatting | bytes 33554432 | tf_op args[1]
  266.5 1.9 fusion.60
  268.4 2.1 fusion.55
  271.6 340.8 %all-to-all-done.1 = f32[32,128,2,512]{1,2,0,3:T(2,128)} async-done(((f32[32,128,2,512]{1,2,0,3:T(2,128)}), f32[32,128,2,512]{1,2,0,3:T(2,128)}, u32[]{:S(2)}, u32[]{:S(2)}) %all-to-all-start.1) | async-done | bytes 16777248 | tf_op jit(solution)/shard_map/all_to_all | solution.py:52
  612.4 11.0 copy.44
  625.2 45.0 %fusion.4 = f32[128,64,2,512,1]{3,0,4,2,1:T(8,128)} fusion(f32[256,128,2,64,1]{1,3,2,0,4:T(8,128)S(1)} %bitcast.91, f32[1,256,2,512]{3,1,2,0:T(8,128)S(1)} %get-tuple-element.8, f32[1,256,2,512]{3,1,2,0:T(8,128)S(1)} %get-tuple-element.7), kind=kOutput, calls=%fused_computation.5 | convolution fusion | flops 25770328064 | bytes 52428800 | tf_op jit(solution)/shard_map/xkpj,pxqa->kjqa/dot_general | solution.py:34
  670.3 33.9 %fusion.7 = f32[128,64,2,256]{3,0,2,1:T(8,128)} fusion(f32[128,64,2,512,1]{3,0,4,2,1:T(8,128)} %fusion.4, f32[128,64,512]{2,0,1:T(8,128)} %copy.48, f32[1,512,2,256]{3,1,0,2:T(8,128)S(1)} %copy-done.2, f32[1,512,2,256]{3,1,0,2:T(8,128)S(1)} %get-tuple-element.5), kind=kOutput, calls=%fused_computation.8 | convolution fusion | flops 25779240960 | bytes 69206016 | tf_op jit(solution)/shard_map/kjqa,qapx->kjpx/dot_general | solution.py:34
  704.2 25.1 %copy.50 = f32[128,64,2,256]{0,2,1,3:T(2,128)} copy(f32[128,64,2,256]{3,0,2,1:T(8,128)} %fusion.7) | data formatting | bytes 33554432 | tf_op jit(solution)/shard_map/kjqa,qapx->kjpx/dot_general | solution.py:34
  729.2 367.8 %all_to_all.72 = f32[128,64,2,256]{0,2,1,3:T(2,128)S(1)} all-to-all(f32[128,64,2,256]{0,2,1,3:T(2,128)} %copy.50), channel_id=1, replica_groups=mesh['row'=4,'col'=8] {'col'}, dimensions={3} | all-to-all | bytes 33554432 | tf_op jit(solution)/shard_map/all_to_all | solution.py:60
  1097.0 10.3 copy.51
  1107.3 7.0 copy.52
  1114.3 32.6 %fusion.13 = f32[128,32,2,256]{3,0,2,1:T(8,128)} fusion(f32[128,512,2,32,1]{0,3,2,1,4:T(8,128)} %bitcast.98, f32[1,512,2,256]{3,1,0,2:T(8,128)S(1)} %copy-done.3, f32[1,512,2,256]{3,1,0,2:T(8,128)S(1)} %get-tuple-element.5), kind=kOutput, calls=%fused_computation.13 | convolution fusion | flops 12885950464 | bytes 27262976 | tf_op jit(solution)/shard_map/kbpx,pbqy->kxqy/dot_general | solution.py:34
  1146.9 13.2 %copy.54 = f32[128,32,2,256]{0,2,1,3:T(2,128)} copy(f32[128,32,2,256]{3,0,2,1:T(8,128)} %fusion.13) | data formatting | bytes 16777216 | tf_op jit(solution)/shard_map/kbpx,pbqy->kxqy/dot_general | solution.py:34
  1160.1 5.7 all-to-all-start.3
  1165.8 2.1 sine_negate_fusion
  1167.9 90.2 %all-to-all-done.3 = f32[128,32,2,256]{0,2,1,3:T(2,128)} async-done(((f32[128,32,2,256]{0,2,1,3:T(2,128)}), f32[128,32,2,256]{0,2,1,3:T(2,128)}, u32[]{:S(2)}, u32[]{:S(2)}) %all-to-all-start.3) | async-done | bytes 8388640 | tf_op jit(solution)/shard_map/all_to_all | solution.py:64
  1258.1 8.4 copy.55
  1266.5 4.9 fusion.22
  (12 shorter events, 3.8 us)
Async XLA Ops:
  0.0 2.1 copy-start
  38.5 99.7 %all-to-all-start = ((f32[4,1,524288]{2,1,0:T(1,128)}), f32[4,1,524288]{2,1,0:T(1,128)}, u32[]{:S(2)}, u32[]{:S(2)}) async-start(f32[4,1,524288]{2,1,0:T(1,128)} %reshape.237), calls=%async_computation | async-start | bytes 16777216 | tf_op jit(solution)/shard_map/all_to_all | solution.py:47
  243.0 369.4 %all-to-all-start.1 = ((f32[32,128,2,512]{1,2,0,3:T(2,128)}), f32[32,128,2,512]{1,2,0,3:T(2,128)}, u32[]{:S(2)}, u32[]{:S(2)}) async-start(f32[32,128,2,512]{1,2,0,3:T(2,128)} %copy.43), calls=%async_computation.1 | async-start | bytes 33554432 | tf_op jit(solution)/shard_map/all_to_all | solution.py:52
  625.2 45.1 %copy-start.2 = (f32[1,512,2,256]{3,1,0,2:T(8,128)S(1)}, f32[1,512,2,256]{3,1,0,2:T(8,128)}, u32[]{:S(2)}) copy-start(f32[1,512,2,256]{3,1,0,2:T(8,128)} %get-tuple-element.6) | copy-start | bytes 3145732
  1107.3 7.0 copy-start.3
  1160.1 97.9 %all-to-all-start.3 = ((f32[128,32,2,256]{0,2,1,3:T(2,128)}), f32[128,32,2,256]{0,2,1,3:T(2,128)}, u32[]{:S(2)}, u32[]{:S(2)}) async-start(f32[128,32,2,256]{0,2,1,3:T(2,128)} %copy.54), calls=%async_computation.3 | async-start | bytes 16777216 | tf_op jit(solution)/shard_map/all_to_all | solution.py:64
  1258.1 13.3 %copy-start.1 = (f32[32,64,256]{2,1,0:T(8,128)S(1)}, f32[32,64,256]{2,1,0:T(8,128)}, u32[]{:S(2)}) copy-start(f32[32,64,256]{2,1,0:T(8,128)} %param.2) | copy-start | bytes 6291460
where the time goes:
time: 1280 us; the launch traced here: 1270 us
  waiting for transfers between devices  523 us (41%)
  blocking collectives  368 us (29%)
  local copies, waits for them, and re-layouts  185 us (14%)
  matrix products  139 us (11%)
  other arithmetic  39.7 us (3%)
  starting transfers between devices  17.2 us (1%)
    all_to_all x1, blocking collectives, on_device(): lax.all_to_all(back_x, 'col', split_axis=3, concat_axis=1, tiled=True)  368 us
    all_to_all x1, waiting for transfers between devices, on_device(): lax.all_to_all(along_y, 'col', split_axis=3, concat_axis=0, tiled=True)  341 us
    dot_general x6, matrix products, contract(): jnp.einsum(pattern, left_side, right_side, precision=lax.Precision.HIGH,...  139 us
    all_to_all x1, waiting for transfers between devices, on_device(): lax.all_to_all(along_z, 'row', split_axis=3, concat_axis=1, tiled=True)  91.6 us
    all_to_all x1, waiting for transfers between devices, on_device(): lax.all_to_all(back_y, 'row', split_axis=3, concat_axis=0, tiled=True)  90.2 us
    dot_general x4, local copies, waits for them, and re-layouts, contract(): jnp.einsum(pattern, left_side, right_side, precision=lax.Precision.HIGH,...  79.7 us
    unnamed x11, local copies, waits for them, and re-layouts  48.9 us
    all_to_all x1, other arithmetic, on_device(): lax.all_to_all(along_z, 'row', split_axis=3, concat_axis=1, tiled=True)  28.2 us
  transfers between devices with their start and end apart: 3, of which 3 were waited for; matrix products, arithmetic and copies ran while one was open for 2% of the time, Pallas kernels for 0%

commit v1 on v0

--- a/solution.py
+++ b/solution.py
@@ -44,7 +44,9 @@
     cosine, sine_part = phases(N, M, M)
     real_table = jnp.stack([cosine, -sine_part], 1)
     along_z = contract("xyz,zqk->xyqk", charge, real_table)
-    by_rows = lax.all_to_all(along_z, "row", split_axis=3, concat_axis=1, tiled=True)
+    pieces = jnp.split(along_z, lax.axis_size("row"), axis=3)
+    received = lax.all_to_all(jnp.stack(pieces), "row", 0, 0)
+    by_rows = jnp.concatenate(received, axis=1)
     forward = forward_table(N, M, M)
     along_y = contract("xypk,pyqb->xkqb", by_rows, forward)
     spectrum = contract(

time: 1280 us -> 1190 us (0.930)
  local copies, waits for them, and re-layouts: 185 us -> 125 us
  other arithmetic: 39.7 us -> 15.1 us
    unnamed x11 -> x9, local copies, waits for them, and re-layouts: 48.9 us -> 17.7 us
    all_to_all x1 -> x0, other arithmetic: 28.2 us -> none  [on_device(): lax.all_to_all(along_z, 'row', split_axis=3, concat_axis=1, tiled=True)]
    all_to_all x3 -> x0, local copies, waits for them, and re-layouts: 18 us -> none  [on_device(): lax.all_to_all(along_z, 'row', split_axis=3, concat_axis=1, tiled=True)]
    dot_general x4 -> x3, local copies, waits for them, and re-layouts: 79.7 us -> 63.3 us  [contract(): jnp.einsum(pattern, left_side, right_side, precision=lax.Precision.HIGH,...]
where the time goes in v1:
time: 1190 us; the launch traced here: 1180 us
  waiting for transfers between devices  523 us (44%)
  blocking collectives  368 us (31%)
  matrix products  137 us (12%)
  local copies, waits for them, and re-layouts  125 us (11%)
  starting transfers between devices  17.5 us (1%)
  other arithmetic  15.1 us (1%)
    all_to_all x1, blocking collectives, on_device(): lax.all_to_all(back_x, 'col', split_axis=3, concat_axis=1, tiled=True)  368 us
    all_to_all x1, waiting for transfers between devices, on_device(): lax.all_to_all(along_y, 'col', split_axis=3, concat_axis=0, tiled=True)  341 us
    dot_general x6, matrix products, contract(): jnp.einsum(pattern, left_side, right_side, precision=lax.Precision.HIGH,...  137 us
    all_to_all x1, waiting for transfers between devices, on_device(): received = lax.all_to_all(jnp.stack(pieces), 'row', 0, 0)  91.6 us
    all_to_all x1, waiting for transfers between devices, on_device(): lax.all_to_all(back_y, 'row', split_axis=3, concat_axis=0, tiled=True)  90.2 us
    dot_general x3, local copies, waits for them, and re-layouts, contract(): jnp.einsum(pattern, left_side, right_side, precision=lax.Precision.HIGH,...  63.3 us
  transfers between devices with their start and end apart: 3, of which 3 were waited for; matrix products, arithmetic and copies ran while one was open for 2% of the time, Pallas kernels for 0%

profile of v1, /device:TPU:0, one launch (start us, length us, event | category | flops | bytes accessed | tf_op | source)
XLA Modules:
  0.0 1184.8 jit_solution(134787478060688913)
XLA Ops:
  0.0 2.1 fusion.58
  2.1 3.7 convolution_bitcast_fusion.1
  5.8 1.0 slice_bitcast_fusion.3
  6.7 3.6 pad_maximum_fusion
  10.4 5.8 all-to-all-start
  16.2 1.9 fusion.57
  18.1 0.3 fusion.34
  18.4 91.6 %all-to-all-done = f32[4,32,64,2,128]{4,2,1,3,0:T(8,128)} async-done(((f32[4,32,64,2,128]{4,2,1,3,0:T(8,128)}), f32[4,32,64,2,128]{4,2,1,3,0:T(8,128)}, u32[]{:S(2)}, u32[]{:S(2)}) %all-to-all-start) | async-done | bytes 8388640 | tf_op jit(solution)/shard_map/all_to_all | solution.py:48
  110.1 4.2 copy.20
  114.3 16.5 %convolution_bitcast_fusion = f32[32,128,2,512]{3,1,2,0:T(8,128)} fusion(f32[32,256,2,128,1]{3,1,2,4,0:T(8,128)S(1)} %bitcast.101, f32[1,256,2,512]{3,1,2,0:T(8,128)S(1)} %get-tuple-element.12, f32[1,256,2,512]{3,1,2,0:T(8,128)S(1)} %get-tuple-element.11), kind=kOutput, calls=%fused_computation.9 | convolution fusion | flops 12885426176 | bytes 27262976 | tf_op jit(solution)/shard_map/xypk,pyqb->xkqb/dot_general | solution.py:34
  130.8 25.1 %copy.23 = f32[32,128,2,512]{1,2,0,3:T(2,128)} copy(f32[32,128,2,512]{3,1,2,0:T(8,128)} %convolution_bitcast_fusion) | data formatting | bytes 33554432 | tf_op jit(solution)/shard_map/xypk,pyqb->xkqb/dot_general | solution.py:34
  155.8 6.0 all-to-all-start.1
  161.8 17.7 %copy.28 = f32[128,64,512]{2,0,1:T(8,128)} copy(f32[128,64,512]{2,1,0:T(8,128)} %param.3) | data formatting | bytes 33554432 | tf_op args[1]
  179.6 1.9 fusion.60
  181.5 2.1 fusion.55
  183.6 1.1 maximum_bitcast_fusion.1
  184.7 340.8 %all-to-all-done.1 = f32[32,128,2,512]{1,2,0,3:T(2,128)} async-done(((f32[32,128,2,512]{1,2,0,3:T(2,128)}), f32[32,128,2,512]{1,2,0,3:T(2,128)}, u32[]{:S(2)}, u32[]{:S(2)}) %all-to-all-start.1) | async-done | bytes 16777248 | tf_op jit(solution)/shard_map/all_to_all | solution.py:54
  525.5 11.0 copy.24
  536.4 1.8 copy.25
  538.3 45.3 %fusion.4 = f32[128,64,2,512,1]{3,0,4,2,1:T(8,128)} fusion(f32[256,128,2,64,1]{1,3,2,0,4:T(8,128)S(1)} %bitcast.96, f32[1,256,2,512]{3,1,2,0:T(8,128)S(1)} %get-tuple-element.12, f32[1,256,2,512]{3,1,2,0:T(8,128)S(1)} %get-tuple-element.11), kind=kOutput, calls=%fused_computation.5 | convolution fusion | flops 25770328064 | bytes 52428800 | tf_op jit(solution)/shard_map/xkpj,pxqa->kjqa/dot_general | solution.py:34
  583.6 33.8 %fusion.7 = f32[128,64,2,256]{3,0,2,1:T(8,128)} fusion(f32[128,64,2,512,1]{3,0,4,2,1:T(8,128)} %fusion.4, f32[128,64,512]{2,0,1:T(8,128)} %copy.28, f32[1,512,2,256]{3,1,0,2:T(8,128)S(1)} %copy-done.2, f32[1,512,2,256]{3,1,0,2:T(8,128)S(1)} %get-tuple-element.9), kind=kOutput, calls=%fused_computation.8 | convolution fusion | flops 25779240960 | bytes 69206016 | tf_op jit(solution)/shard_map/kjqa,qapx->kjpx/dot_general | solution.py:34
  617.4 25.0 %copy.30 = f32[128,64,2,256]{0,2,1,3:T(2,128)} copy(f32[128,64,2,256]{3,0,2,1:T(8,128)} %fusion.7) | data formatting | bytes 33554432 | tf_op jit(solution)/shard_map/kjqa,qapx->kjpx/dot_general | solution.py:34
  642.4 367.8 %all_to_all.59 = f32[128,64,2,256]{0,2,1,3:T(2,128)S(1)} all-to-all(f32[128,64,2,256]{0,2,1,3:T(2,128)} %copy.30), channel_id=1, replica_groups=mesh['row'=4,'col'=8] {'col'}, dimensions={3} | all-to-all | bytes 33554432 | tf_op jit(solution)/shard_map/all_to_all | solution.py:62
  1010.1 10.3 copy.31
  1020.4 7.0 copy.32
  1027.4 32.5 %fusion.13 = f32[128,32,2,256]{3,0,2,1:T(8,128)} fusion(f32[128,512,2,32,1]{0,3,2,1,4:T(8,128)} %bitcast.100, f32[1,512,2,256]{3,1,0,2:T(8,128)S(1)} %copy-done.3, f32[1,512,2,256]{3,1,0,2:T(8,128)S(1)} %get-tuple-element.9), kind=kOutput, calls=%fused_computation.14 | convolution fusion | flops 12885950464 | bytes 27262976 | tf_op jit(solution)/shard_map/kbpx,pbqy->kxqy/dot_general | solution.py:34
  1059.9 13.2 %copy.34 = f32[128,32,2,256]{0,2,1,3:T(2,128)} copy(f32[128,32,2,256]{3,0,2,1:T(8,128)} %fusion.13) | data formatting | bytes 16777216 | tf_op jit(solution)/shard_map/kbpx,pbqy->kxqy/dot_general | solution.py:34
  1073.2 5.7 all-to-all-start.3
  1078.8 2.1 sine_negate_fusion
  1080.9 90.2 %all-to-all-done.3 = f32[128,32,2,256]{0,2,1,3:T(2,128)} async-done(((f32[128,32,2,256]{0,2,1,3:T(2,128)}), f32[128,32,2,256]{0,2,1,3:T(2,128)}, u32[]{:S(2)}, u32[]{:S(2)}) %all-to-all-start.3) | async-done | bytes 8388640 | tf_op jit(solution)/shard_map/all_to_all | solution.py:66
  1171.1 8.4 copy.35
  1179.5 4.9 fusion.22
  (8 shorter events, 0.0 us)
Async XLA Ops:
  0.0 2.1 copy-start
  10.4 99.7 %all-to-all-start = ((f32[4,32,64,2,128]{4,2,1,3,0:T(8,128)}), f32[4,32,64,2,128]{4,2,1,3,0:T(8,128)}, u32[]{:S(2)}, u32[]{:S(2)}) async-start(f32[4,32,64,2,128]{4,2,1,3,0:T(8,128)} %pad_maximum_fusion), calls=%async_computation | async-start | bytes 16777216 | tf_op jit(solution)/shard_map/all_to_all | solution.py:48
  155.8 369.6 %all-to-all-start.1 = ((f32[32,128,2,512]{1,2,0,3:T(2,128)}), f32[32,128,2,512]{1,2,0,3:T(2,128)}, u32[]{:S(2)}, u32[]{:S(2)}) async-start(f32[32,128,2,512]{1,2,0,3:T(2,128)} %copy.23), calls=%async_computation.1 | async-start | bytes 33554432 | tf_op jit(solution)/shard_map/all_to_all | solution.py:54
  538.2 45.3 %copy-start.2 = (f32[1,512,2,256]{3,1,0,2:T(8,128)S(1)}, f32[1,512,2,256]{3,1,0,2:T(8,128)}, u32[]{:S(2)}) copy-start(f32[1,512,2,256]{3,1,0,2:T(8,128)} %get-tuple-element.10) | copy-start | bytes 3145732
  1020.4 7.0 copy-start.3
  1073.2 97.9 %all-to-all-start.3 = ((f32[128,32,2,256]{0,2,1,3:T(2,128)}), f32[128,32,2,256]{0,2,1,3:T(2,128)}, u32[]{:S(2)}, u32[]{:S(2)}) async-start(f32[128,32,2,256]{0,2,1,3:T(2,128)} %copy.34), calls=%async_computation.3 | async-start | bytes 16777216 | tf_op jit(solution)/shard_map/all_to_all | solution.py:66
  1171.1 13.3 %copy-start.1 = (f32[32,64,256]{2,1,0:T(8,128)S(1)}, f32[32,64,256]{2,1,0:T(8,128)}, u32[]{:S(2)}) copy-start(f32[32,64,256]{2,1,0:T(8,128)} %param.2) | copy-start | bytes 6291460
